TPU v7x, 32 devices: a whole 2x2x4 slice. The times are simulated.
32 devices in a mesh: groups: 2 (over y), seq: 4 (over z), head: 2 (over x), rep: 2 (over core).
Axes of the slice: x: 2, y: 2, z: 4, core: 2. Of those that a mesh axis runs over, the one named last changes fastest.
Arguments:
- queries: bfloat16 [128, 64, 128], P(('groups', 'seq', 'rep'), 'head'), parts along dimension 0, may hold values from -256 to 256
- page_owner: int32 [128, 128], P(('groups', 'seq', 'rep')), parts along dimension 0, may hold values from -1 to 3, as said below
- page_slot: int32 [128, 128], P(('groups', 'seq', 'rep')), parts along dimension 0, may hold values from -1 to 63, as said below
- lengths: int32 [128], P(('groups', 'seq', 'rep')), parts along dimension 0, may hold values from 1 to 16384, as said below
- keys: bfloat16 [1024, 8, 128, 128], P(('groups', 'seq', 'rep'), 'head'), parts along dimension 0, may hold values from -24 to 24
- values: bfloat16 [1024, 8, 128, 128], P(('groups', 'seq', 'rep'), 'head'), parts along dimension 0, may hold values from -6 to 6
Outputs:
- attended: bfloat16 [128, 64, 128], P(('groups', 'seq', 'rep'), 'head'), parts along dimension 0
There are 2 independent parts, one for each index of `groups`. A program takes and returns all parts, laid end to end along the dimension named above; each array names one. Nothing has to cross between parts.
Inputs may be any that keep to these rules, and one draw needn't show every extreme that they name: `page_owner`: for j below ceil(lengths[r] / 128) the seq index of the device, among those of r's half (r // 8) % 2, whose pool holds page j of r; -1 for later j. `page_slot`: the page's slot in that pool, -1 where page_owner is -1. No slot of a pool holds two pages; in each half, some device's pool has all 64 slots in use. `lengths`: in each half some request has the most.
All inputs are finite; a program needn't handle non-finite values.
Results may differ from a plain program's by a relative error of at most 0.0041.
Values may be sent and summed in bfloat16 or wider, within the bound.
A program may use at most 64 MiB of HBM per device.

v0:
```python
import math

import jax
import jax.numpy as jnp
from jax import lax
from jax.sharding import PartitionSpec as P

masked_score = -1e30


def on_device(queries, page_owner, page_slot, lengths, keys, values):
    rows_own = queries.shape[0]
    head_count = queries.shape[1]
    head_width = queries.shape[2]
    pool_size = keys.shape[0]
    kv_heads = keys.shape[1]
    page_tokens = keys.shape[2]
    group_size = head_count // kv_heads
    most_pages = page_owner.shape[1]
    page_index = jnp.arange(most_pages, dtype=jnp.int32)
    all_queries, all_owner, all_slot, all_length = (
        lax.all_gather(queries, "seq", axis=0, tiled=True),
        lax.all_gather(page_owner, "seq", axis=0, tiled=True),
        lax.all_gather(page_slot, "seq", axis=0, tiled=True),
        lax.all_gather(lengths, "seq", axis=0, tiled=True),
    )
    live_count = jnp.clip(all_length[:, None] - page_index[None, :] * page_tokens, 0, page_tokens)
    rows_half = all_queries.shape[0]
    seq_index = lax.axis_index("seq")
    held_here = (all_owner == seq_index) & (live_count > 0)
    slot_index = jnp.arange(pool_size, dtype=jnp.int32)
    matches = held_here[None, :, :] & (all_slot[None, :, :] == slot_index[:, None, None])
    slot_owner = jnp.any(matches, axis=2)
    slot_tokens = jnp.sum(jnp.where(matches, live_count[None, :, :], 0), axis=(1, 2))
    picker = slot_owner.astype(jnp.bfloat16)
    flat_queries = all_queries.reshape(rows_half, head_count * head_width)
    slot_queries = jnp.dot(picker, flat_queries, preferred_element_type=jnp.float32)
    slot_queries = slot_queries.astype(jnp.bfloat16).reshape(
        pool_size, kv_heads, group_size, head_width
    )
    score_scale = 1.0 / math.sqrt(head_width)
    scores = (
        jnp.einsum("pkgd,pktd->pkgt", slot_queries, keys, preferred_element_type=jnp.float32)
        * score_scale
    )
    token_index = jnp.arange(page_tokens, dtype=jnp.int32)
    live_tokens = (token_index[None, :] < slot_tokens[:, None])[:, None, None, :]
    scores = jnp.where(live_tokens, scores, masked_score)
    page_max = jnp.max(scores, axis=3)
    weights = jnp.where(live_tokens, jnp.exp(scores - page_max[..., None]), 0.0)
    page_sum = jnp.sum(weights, axis=3)
    page_out = jnp.einsum(
        "pkgt,pktd->pkgd", weights.astype(jnp.bfloat16), values, preferred_element_type=jnp.float32
    )
    linked = slot_owner.T[:, :, None, None]
    request_max = jnp.max(jnp.where(linked, page_max[None], masked_score), axis=1)
    rescale = jnp.where(
        linked, jnp.exp(jnp.minimum(page_max[None] - request_max[:, None], 0.0)), 0.0
    )
    request_sum = jnp.sum(rescale * page_sum[None], axis=1)
    request_out = jnp.einsum("rpkg,pkgd->rkgd", rescale, page_out, precision=lax.Precision.HIGHEST)
    got_max, got_sum, got_out = (
        lax.all_to_all(request_max, "seq", split_axis=0, concat_axis=0, tiled=True),
        lax.all_to_all(request_sum, "seq", split_axis=0, concat_axis=0, tiled=True),
        lax.all_to_all(request_out, "seq", split_axis=0, concat_axis=0, tiled=True),
    )
    sources = rows_half // rows_own
    got_max = got_max.reshape((sources, rows_own) + got_max.shape[1:])
    got_sum = got_sum.reshape((sources, rows_own) + got_sum.shape[1:])
    got_out = got_out.reshape((sources, rows_own) + got_out.shape[1:])
    overall = jnp.max(got_max, axis=0)
    source_scale = jnp.exp(got_max - overall[None])
    own_sum = jnp.sum(source_scale * got_sum, axis=0)
    own_out = jnp.sum(source_scale[..., None] * got_out, axis=0)
    attended = own_out / own_sum[..., None]
    return attended.astype(jnp.bfloat16).reshape(rows_own, head_count, head_width)


def solution(mesh):
    placed = (
        P(("groups", "seq", "rep"), "head", None),
        P(("groups", "seq", "rep"), None),
        P(("groups", "seq", "rep"), None),
        P(("groups", "seq", "rep")),
        P(("groups", "seq", "rep"), "head", None, None),
        P(("groups", "seq", "rep"), "head", None, None),
    )
    return jax.shard_map(
        on_device,
        mesh=mesh,
        in_specs=placed,
        out_specs=P(("groups", "seq", "rep"), "head", None),
        check_vma=False,
    )
```

profile of v0, /device:TPU:0, one launch (start us, length us, event | category | flops | bytes accessed | tf_op | source)
XLA Modules:
  0.0 100.2 jit_solution(10780645562737073349)
XLA Ops:
  0.0 1.2 %dynamic-slice = u32[1]{0:T(128)} dynamic-slice(u32[32]{0:T(128)} %constant.28, u32[]{:T(128)S(6)} %add), dynamic_slice_sizes={1} | dynamic-slice | bytes 12
  1.9 0.9 dynamic-update-slice
  2.8 9.9 %all-reduce = s32[32]{0:T(128)S(1)} all-reduce(s32[32]{0:T(128)S(1)} %dynamic-update-slice), channel_id=1, replica_groups=mesh['groups'=2,'seq'=4,'head'=2,'rep'=2] {'seq'}, use_global_device_ids=true, to_apply=%add | all-reduce | flops 32 | bytes 256
  12.7 13.3 %all_gather.12 = s32[32,128]{1,0:T(8,128)S(1)} all-gather(s32[8,128]{1,0:T(8,128)} %param.7), channel_id=1, replica_groups=mesh['groups'=2,'seq'=4,'head'=2,'rep'=2] {'seq'}, dimensions={0}, use_global_device_ids=true | all-gather | bytes 20480 | tf_op jit(solution)/shard_map/all_gather | solution.py:23
  26.0 13.3 %all_gather.14 = s32[32,128]{1,0:T(8,128)S(1)} all-gather(s32[8,128]{1,0:T(8,128)} %param.8), channel_id=1, replica_groups=mesh['groups'=2,'seq'=4,'head'=2,'rep'=2] {'seq'}, dimensions={0}, use_global_device_ids=true | all-gather | bytes 20480 | tf_op jit(solution)/shard_map/all_gather | solution.py:24
  39.5 1.2 %fusion.4 = pred[64,32]{1,0:T(8,128)(4,1)S(1)} fusion(s32[32,128]{1,0:T(8,128)S(1)} %all_gather.14, pred[32,128]{1,0:T(8,128)(4,1)S(1)} %compare_and_fusion), kind=kLoop, calls=%fused_computation.10 | loop fusion | flops 784384 | bytes 22528 | tf_op jit(solution)/shard_map/reduce_or | solution.py:33
  40.7 1.2 %select_reduce_fusion = s32[64]{0:T(128)S(1)} fusion(s32[32,128]{1,0:T(8,128)S(1)} %subtract_clamp_fusion, s32[32,128]{1,0:T(8,128)S(1)} %all_gather.14, pred[32,128]{1,0:T(8,128)(4,1)S(1)} %compare_and_fusion), kind=kLoop, calls=%fused_computation.7 | loop fusion | flops 1048512 | bytes 37120 | tf_op jit(solution)/shard_map/reduce_sum | solution.py:34
  42.0 14.0 %all_gather.15 = bf16[32,32,128]{2,1,0:T(8,128)(2,1)S(1)} all-gather(bf16[8,32,128]{2,1,0:T(8,128)(2,1)} %param.6), channel_id=1, replica_groups=mesh['groups'=2,'seq'=4,'head'=2,'rep'=2] {'seq'}, dimensions={0}, use_global_device_ids=true | all-gather | bytes 327680 | tf_op jit(solution)/shard_map/all_gather | solution.py:22
  56.0 0.3 fusion.1
  56.4 6.9 %fusion.22 = (f32[64,4,8]{2,1,0:T(4,128)S(1)}, f32[64,4,8,128]{3,2,1,0:T(8,128)S(1)}) fusion(bf16[64,4,8,128]{3,2,1,0:T(8,128)(2,1)S(1)} %bitcast.21, bf16[64,4,128,128]{3,2,1,0:T(8,128)(2,1)} %param.10, pred[64,128]{1,0:T(8,128)(4,1)S(1)} %iota_compare_fusion.1), kind=kOutput, calls=%fused_computation.38 | convolution fusion | flops 67893248 | bytes 9977856 | tf_op jit(solution)/shard_map/pkgd,pktd->pkgt/dot_general | solution.py:43
  63.4 0.8 fusion.5
  64.4 0.2 select_reduce_fusion.1
  64.6 0.4 multiply_reduce_fusion
  65.1 0.7 reshape.94
  65.8 3.2 %all-to-all-start.2 = ((f32[4,1,256]{2,1,0:T(1,128)}), f32[4,1,256]{2,1,0:T(1,128)S(1)}, u32[]{:S(2)}, u32[]{:S(2)}) async-start(f32[4,1,256]{2,1,0:T(1,128)} %reshape.94), calls=%async_computation.2 | async-start | bytes 8192 | tf_op jit(solution)/shard_map/all_to_all | solution.py:64
  69.1 4.7 %fusion.7 = f32[64,4,8,128]{3,2,1,0:T(8,128)S(1)} fusion(bf16[64,4,128,128]{3,2,1,0:T(8,128)(2,1)} %param.11, f32[64,4,8,128]{3,2,1,0:T(8,128)S(1)} %get-tuple-element.8, f32[64,4,8]{2,1,0:T(4,128)S(1)} %get-tuple-element.7, pred[64,128]{1,0:T(8,128)(4,1)S(1)} %iota_compare_fusion.1), kind=kOutput, calls=%fused_computation.13 | convolution fusion | flops 67895296 | bytes 10502144 | tf_op jit(solution)/shard_map/pkgt,pktd->pkgd/dot_general | solution.py:52
  73.9 0.7 reshape.92
  74.6 5.0 %all-to-all-start = ((f32[4,1,256]{2,1,0:T(1,128)}), f32[4,1,256]{2,1,0:T(1,128)S(1)}, u32[]{:S(2)}, u32[]{:S(2)}) async-start(f32[4,1,256]{2,1,0:T(1,128)} %reshape.92), calls=%async_computation | async-start | bytes 8192 | tf_op jit(solution)/shard_map/all_to_all | solution.py:63
  79.7 1.6 %convolution_bitcast_fusion = f32[32,4,8,128]{3,0,2,1:T(8,128)S(1)} fusion(f32[64,4,8,128]{3,2,1,0:T(8,128)S(1)} %fusion.7, f32[32,4,8]{0,2,1:T(8,128)S(1)} %select_reduce_fusion.1, f32[64,4,8]{0,2,1:T(8,128)S(1)} %copy.30, pred[32,64]{1,0:T(8,128)(4,1)S(1)} %copy.29), kind=kOutput, calls=%fused_computation.4 | convolution fusion | flops 100859904 | bytes 1587200 | tf_op jit(solution)/shard_map/rpkg,pkgd->rkgd/dot_general | solution.py:61
  81.3 1.1 %copy.35 = f32[32,4,8,128]{3,2,1,0:T(8,128)} copy(f32[32,4,8,128]{3,0,2,1:T(8,128)S(1)} %convolution_bitcast_fusion) | data formatting | bytes 1048576 | tf_op jit(solution)/shard_map/rpkg,pkgd->rkgd/transpose | solution.py:61
  82.4 2.9 %all-to-all-done = f32[4,1,256]{2,1,0:T(1,128)S(1)} async-done(((f32[4,1,256]{2,1,0:T(1,128)}), f32[4,1,256]{2,1,0:T(1,128)S(1)}, u32[]{:S(2)}, u32[]{:S(2)}) %all-to-all-start) | async-done | bytes 4128 | tf_op jit(solution)/shard_map/all_to_all | solution.py:63
  85.3 3.5 %all-to-all-start.1 = ((f32[32,4,8,128]{3,2,1,0:T(8,128)}), f32[32,4,8,128]{3,2,1,0:T(8,128)S(1)}, u32[]{:S(2)}, u32[]{:S(2)}) async-start(f32[32,4,8,128]{3,2,1,0:T(8,128)} %copy.35), calls=%async_computation.1 | async-start | bytes 1048576 | tf_op jit(solution)/shard_map/all_to_all | solution.py:65
  88.8 0.5 broadcast.55
  89.3 0.7 reduce
  90.0 0.1 reshape.95
  90.1 0.1 copy.39
  90.2 0.7 reduce.1
  90.9 0.1 reshape.93
  91.0 0.1 copy.33
  91.4 7.7 %all-to-all-done.1 = f32[32,4,8,128]{3,2,1,0:T(8,128)S(1)} async-done(((f32[32,4,8,128]{3,2,1,0:T(8,128)}), f32[32,4,8,128]{3,2,1,0:T(8,128)S(1)}, u32[]{:S(2)}, u32[]{:S(2)}) %all-to-all-start.1) | async-done | bytes 524320 | tf_op jit(solution)/shard_map/all_to_all | solution.py:65
  99.1 0.3 fusion.9
  99.4 0.7 fusion.19
  (16 shorter events, 1.0 us)
Async XLA Ops:
  65.8 8.8 %all-to-all-start.2 = ((f32[4,1,256]{2,1,0:T(1,128)}), f32[4,1,256]{2,1,0:T(1,128)S(1)}, u32[]{:S(2)}, u32[]{:S(2)}) async-start(f32[4,1,256]{2,1,0:T(1,128)} %reshape.94), calls=%async_computation.2 | async-start | bytes 8192 | tf_op jit(solution)/shard_map/all_to_all | solution.py:64
  74.6 10.7 %all-to-all-start = ((f32[4,1,256]{2,1,0:T(1,128)}), f32[4,1,256]{2,1,0:T(1,128)S(1)}, u32[]{:S(2)}, u32[]{:S(2)}) async-start(f32[4,1,256]{2,1,0:T(1,128)} %reshape.92), calls=%async_computation | async-start | bytes 8192 | tf_op jit(solution)/shard_map/all_to_all | solution.py:63
  85.3 13.7 %all-to-all-start.1 = ((f32[32,4,8,128]{3,2,1,0:T(8,128)}), f32[32,4,8,128]{3,2,1,0:T(8,128)S(1)}, u32[]{:S(2)}, u32[]{:S(2)}) async-start(f32[32,4,8,128]{3,2,1,0:T(8,128)} %copy.35), calls=%async_computation.1 | async-start | bytes 1048576 | tf_op jit(solution)/shard_map/all_to_all | solution.py:65
where the time goes:
time: 101 us; the launch traced here: 100 us
  blocking collectives  50.6 us (50%)
  matrix products  13.6 us (13%)
  starting transfers between devices  11.8 us (12%)
  waiting for transfers between devices  10.6 us (10%)
  other arithmetic  6.56 us (6%)
  local copies, waits for them, and re-layouts  6.25 us (6%)
    all_gather x1, blocking collectives, on_device(): lax.all_gather(queries, 'seq', axis=0, tiled=True)  14 us
    all_gather x1, blocking collectives, on_device(): lax.all_gather(page_slot, 'seq', axis=0, tiled=True)  13.3 us
    all_gather x1, blocking collectives, on_device(): lax.all_gather(page_owner, 'seq', axis=0, tiled=True)  13.3 us
    unnamed x1, blocking collectives  9.92 us
    all_to_all x1, waiting for transfers between devices, on_device(): lax.all_to_all(request_out, 'seq', split_axis=0, concat_axis=0, tiled=True)  7.67 us
    dot_general x1, matrix products, on_device(): jnp.einsum('pkgd,pktd->pkgt', slot_queries, keys, preferred_element_type=...  6.94 us
    all_to_all x1, starting transfers between devices, on_device(): lax.all_to_all(request_max, 'seq', split_axis=0, concat_axis=0, tiled=True)  5.04 us
    dot_general x1, matrix products, on_device(): jnp.einsum('pkgt,pktd->pkgd', weights.astype(jnp.bfloat16), values, prefe...  4.72 us
  transfers between devices with their start and end apart: 3, of which 2 were waited for; matrix products, arithmetic and copies ran while one was open for 11% of the time, Pallas kernels for 0%

commit v1 on v0

v1 whole, which is shorter than its diff:
```python
import functools
import math

import jax
import jax.numpy as jnp
from jax import lax
from jax.experimental import pallas as pl
from jax.experimental.pallas import tpu as pltpu
from jax.sharding import PartitionSpec as P

MASKED = -1e30
F32 = jnp.float32
BF16 = jnp.bfloat16
NT = (((1,), (1,)), ((), ()))


def iota(shape, dim):
    return lax.broadcasted_iota(jnp.int32, shape, dim)


def kernel(
    n, unroll, lens_ref, q_ref, owner_ref, slot_ref, k_hbm, v_hbm, out_ref,
    kbuf, vbuf, qall, tsend, trecv, liveb, reqb, mt, m, qslot, pmb, lb, oacc, ohi,
    osend, orecv, ssend, srecv,
    ksem, vsem, tss, trs, qss, qrs, oss, ors, sss, srs,
):
    pool, kv, tokens, width = k_hbm.shape
    rows = q_ref.shape[0]
    group = q_ref.shape[1] // kv
    block = rows * group
    lanes = trecv.shape[2]
    scale = 1.0 / math.sqrt(width)
    me = lax.axis_index("seq")

    def peer(off):
        return {"seq": lax.rem(me + off, n)}

    def source(off):
        return {"seq": lax.rem(me + n - off, n)}

    def remote(src, dst, ssem, rsem, to):
        return pltpu.make_async_remote_copy(
            src_ref=src, dst_ref=dst, send_sem=ssem, recv_sem=rsem,
            device_id=to, device_id_type=pl.DeviceIdType.MESH,
        )

    barrier = pltpu.get_barrier_semaphore()
    for off in range(1, n):
        pl.semaphore_signal(
            barrier, inc=1, device_id=peer(off), device_id_type=pl.DeviceIdType.MESH
        )
    kcopies = [pltpu.make_async_copy(k_hbm.at[:, h], kbuf.at[h], ksem.at[h]) for h in range(kv)]
    vcopies = [pltpu.make_async_copy(v_hbm.at[:, h], vbuf.at[h], vsem.at[h]) for h in range(kv)]
    for h in range(kv):
        kcopies[h].start()
        vcopies[h].start()

    queries = q_ref[...].astype(F32).reshape(rows, kv, group, width)
    for h in range(kv):
        qall[h, 0:block, :] = queries[:, h].reshape(block, width).astype(BF16)

    span = owner_ref.shape[1]
    row = iota((rows, span), 0)
    length = jnp.zeros((rows, span), jnp.int32)
    for r in range(rows):
        length = jnp.where(row == r, lens_ref[r], length)
    live = jnp.clip(length - iota((rows, span), 1) * tokens, 0, tokens)
    live_f = live.astype(F32)
    owner = owner_ref[...]
    slot = slot_ref[...]
    ones = jnp.ones((8, span), BF16)
    slot_id = iota((pool, span), 0)
    for off in range(n):
        there = lax.rem(me + off, n)
        key = jnp.where((owner == there) & (live > 0), slot, -1)
        acc_live = jnp.zeros((pool, span), F32)
        acc_req = jnp.zeros((pool, span), F32)
        for r in range(rows):
            hit = slot_id == key[r : r + 1, :]
            acc_live = jnp.where(hit, live_f[r : r + 1, :], acc_live)
            acc_req = jnp.where(hit, float(r + 1), acc_req)
        t_live = lax.dot_general(ones, acc_live.astype(BF16), NT, preferred_element_type=F32)
        t_req = lax.dot_general(ones, acc_req.astype(BF16), NT, preferred_element_type=F32)
        table = jnp.where(iota((8, pool), 0) == 0, t_live, t_req)
        if lanes > pool:
            table = jnp.concatenate([table, jnp.zeros((8, lanes - pool), F32)], axis=1)
        if off == 0:
            trecv[0] = table
        else:
            tsend[off] = table

    pl.semaphore_wait(barrier, n - 1)
    tcopies = {}
    qcopies = {}
    for off in range(1, n):
        tcopies[off] = remote(
            tsend.at[off], trecv.at[off], tss.at[off], trs.at[off], peer(off)
        )
        tcopies[off].start()
    for h in range(kv):
        for off in range(1, n):
            qcopies[h, off] = remote(
                qall.at[h, pl.ds(0, block)],
                qall.at[h, pl.ds(off * block, block)],
                qss.at[h, off], qrs.at[h, off], peer(off),
            )
            qcopies[h, off].start()

    for off in range(1, n):
        tcopies[off].wait_recv()
    live_row = trecv[0][0:1, :]
    req_row = trecv[0][1:2, :]
    for off in range(1, n):
        t = trecv[off]
        live_row = live_row + t[0:1, :]
        req_row = req_row + jnp.where(t[1:2, :] > 0.0, t[1:2, :] + float(off * rows), 0.0)
    pg = pool * group
    spread = jnp.where(iota((pg, lanes), 0) // group == iota((pg, lanes), 1), 1.0, 0.0)
    spread = spread.astype(BF16)
    liveb[...] = lax.dot_general(
        spread, jnp.broadcast_to(live_row, (128, lanes)).astype(BF16), NT,
        preferred_element_type=F32,
    )
    reqb[...] = lax.dot_general(
        spread, jnp.broadcast_to(req_row, (128, lanes)).astype(BF16), NT,
        preferred_element_type=F32,
    )
    same = iota((pg, 128), 0) % group == iota((pg, 128), 1) % group
    for c in range(n * block // 128):
        want = ((iota((pg, 128), 1) + c * 128) // group + 1).astype(F32)
        mt[:, c * 128 : (c + 1) * 128] = jnp.where(
            same & (reqb[...] == want), 1.0, 0.0
        ).astype(BF16)
    spread_t = jnp.where(iota((lanes, pg), 0) == iota((lanes, pg), 1) // group, 1.0, 0.0)
    req_wide = jnp.dot(
        jnp.broadcast_to(req_row, (8, lanes)).astype(BF16), spread_t.astype(BF16),
        preferred_element_type=F32,
    )[0:1, :]
    same_t = iota((block, pg), 0) % group == iota((block, pg), 1) % group
    for off in range(n):
        want = (iota((block, pg), 0) // group + (off * rows + 1)).astype(F32)
        m[off * block : (off + 1) * block, :] = jnp.where(
            same_t & (req_wide == want), 1.0, 0.0
        ).astype(BF16)

    lane_f = iota((group, 128), 1).astype(F32)
    tops = []
    sums = []
    ocopies = {}
    for h in range(kv):
        for off in range(1, n):
            qcopies[h, off].wait_recv()
        qslot[...] = jnp.dot(mt[...], qall[h], preferred_element_type=F32)
        kcopies[h].wait()
        vcopies[h].wait()

        def pages(i, top):
            for u in range(unroll):
                p = i * unroll + u
                at = pl.ds(pl.multiple_of(p * group, group), group)
                s = lax.dot_general(
                    qslot[at, :].astype(BF16), kbuf[h, p], NT, preferred_element_type=F32
                )
                s = jnp.where(lane_f < liveb[at, :], s * scale, MASKED)
                pm = jnp.max(s, axis=1, keepdims=True)
                w = jnp.exp(s - pm)
                total = jnp.sum(w, axis=1, keepdims=True)
                oacc[at, :] = jnp.dot(w.astype(BF16), vbuf[h, p], preferred_element_type=F32)
                pmb[at, :] = jnp.broadcast_to(pm, (group, 128))
                lb[at, :] = jnp.broadcast_to(total, (group, 128))
                top = jnp.maximum(top, jnp.where(reqb[at, :] == lane_f + 1.0, pm, MASKED))
            return top

        top = lax.fori_loop(0, pool // unroll, pages, jnp.full((group, 128), MASKED, F32))

        def merge(i, acc):
            for u in range(unroll):
                p = i * unroll + u
                at = pl.ds(pl.multiple_of(p * group, group), group)
                mine = reqb[at, :] == lane_f + 1.0
                rm = jnp.max(jnp.where(mine, top, MASKED), axis=1, keepdims=True)
                sc = jnp.exp(jnp.minimum(pmb[at, :] - rm, 0.0))
                ohi[at, :] = oacc[at, :] * sc
                acc = acc + jnp.where(mine, sc * lb[at, :], 0.0)
            return acc

        acc = lax.fori_loop(0, pool // unroll, merge, jnp.zeros((group, 128), F32))
        osend[h] = jnp.dot(
            m[...], ohi[...].astype(BF16), preferred_element_type=F32
        ).astype(BF16)
        for off in range(1, n):
            ocopies[h, off] = remote(
                osend.at[h, pl.ds(off * block, block)], orecv.at[h, off],
                oss.at[h, off], ors.at[h, off], source(off),
            )
            ocopies[h, off].start()
        tops.append(top)
        sums.append(acc)

    lane = iota((group, 128), 1)
    scopies = {}
    for off in range(n):
        stat = jnp.zeros((group, 128), F32)
        for h in range(kv):
            for j, x in enumerate((tops[h], sums[h])):
                at = (2 * h + j) * rows
                shift = (at - off * rows) % 128
                y = pltpu.roll(x, shift, 1) if shift else x
                stat = jnp.where((lane >= at) & (lane < at + rows), y, stat)
        if off == 0:
            srecv[0] = stat
        else:
            ssend[off] = stat
            scopies[off] = remote(
                ssend.at[off], srecv.at[off], sss.at[off], srs.at[off], source(off)
            )
            scopies[off].start()

    for off in range(1, n):
        scopies[off].wait_recv()
    stats = [srecv[off] for off in range(n)]
    best = functools.reduce(jnp.maximum, stats)
    factors = [jnp.exp(x - best) for x in stats]
    whole = functools.reduce(
        jnp.add, [f * pltpu.roll(x, 128 - rows, 1) for f, x in zip(factors, stats)]
    )
    factors = [f / whole for f in factors]
    parts = []
    for h in range(kv):
        gathered = []
        for off in range(n):
            if off == 0:
                got = osend[h, 0:block, :]
            else:
                ocopies[h, off].wait_recv()
                got = orecv[h, off]
            gathered.append(got.astype(F32).reshape(rows, group, width))
        per_row = []
        for r in range(rows):
            at = 2 * h * rows + r
            total = factors[0][:, at : at + 1] * gathered[0][r]
            for off in range(1, n):
                total = total + factors[off][:, at : at + 1] * gathered[off][r]
            per_row.append(total)
        parts.append(per_row)
    for r in range(rows):
        out_ref[r] = jnp.concatenate([parts[h][r] for h in range(kv)], axis=0).astype(BF16)

    for off in range(1, n):
        tcopies[off].wait_send()
        scopies[off].wait_send()
        for h in range(kv):
            qcopies[h, off].wait_send()
            ocopies[h, off].wait_send()


def on_device(n, queries, page_owner, page_slot, lengths, keys, values):
    pool, kv, tokens, width = keys.shape
    rows, heads, _ = queries.shape
    group = heads // kv
    block = rows * group
    pg = pool * group
    lanes = -(-pool // 128) * 128
    unroll = math.gcd(pool, 16)
    dma = pltpu.SemaphoreType.DMA
    vmem = pl.BlockSpec(memory_space=pltpu.VMEM)
    return pl.pallas_call(
        functools.partial(kernel, n, unroll),
        out_shape=jax.ShapeDtypeStruct(queries.shape, BF16),
        in_specs=[
            pl.BlockSpec(memory_space=pltpu.SMEM),
            vmem,
            vmem,
            vmem,
            pl.BlockSpec(memory_space=pl.ANY),
            pl.BlockSpec(memory_space=pl.ANY),
        ],
        out_specs=vmem,
        scratch_shapes=[
            pltpu.VMEM((kv, pool, tokens, width), BF16),
            pltpu.VMEM((kv, pool, tokens, width), BF16),
            pltpu.VMEM((kv, n * block, width), BF16),
            pltpu.VMEM((n, 8, lanes), F32),
            pltpu.VMEM((n, 8, lanes), F32),
            pltpu.VMEM((pg, 128), F32),
            pltpu.VMEM((pg, 128), F32),
            pltpu.VMEM((pg, n * block), BF16),
            pltpu.VMEM((n * block, pg), BF16),
            pltpu.VMEM((pg, width), F32),
            pltpu.VMEM((pg, 128), F32),
            pltpu.VMEM((pg, 128), F32),
            pltpu.VMEM((pg, width), F32),
            pltpu.VMEM((pg, width), F32),
            pltpu.VMEM((kv, n * block, width), BF16),
            pltpu.VMEM((kv, n, block, width), BF16),
            pltpu.VMEM((n, group, 128), F32),
            pltpu.VMEM((n, group, 128), F32),
            dma((kv,)), dma((kv,)),
            dma((n,)), dma((n,)),
            dma((kv, n)), dma((kv, n)),
            dma((kv, n)), dma((kv, n)),
            dma((n,)), dma((n,)),
        ],
        compiler_params=pltpu.CompilerParams(
            collective_id=0, has_side_effects=True, vmem_limit_bytes=60 * 1024 * 1024
        ),
        name="paged",
    )(lengths, queries, page_owner, page_slot, keys, values)


def solution(mesh):
    placed = (
        P(("groups", "seq", "rep"), "head", None),
        P(("groups", "seq", "rep"), None),
        P(("groups", "seq", "rep"), None),
        P(("groups", "seq", "rep")),
        P(("groups", "seq", "rep"), "head", None, None),
        P(("groups", "seq", "rep"), "head", None, None),
    )
    return jax.shard_map(
        functools.partial(on_device, mesh.shape["seq"]),
        mesh=mesh,
        in_specs=placed,
        out_specs=P(("groups", "seq", "rep"), "head", None),
        check_vma=False,
    )
```

time: 101 us -> 83.5 us (0.83)
  Pallas kernels: 0 us -> 81.9 us
  blocking collectives: 50.6 us -> 0 us
  matrix products: 13.6 us -> 0 us
  starting transfers between devices: 11.8 us -> 0 us
  waiting for transfers between devices: 10.6 us -> 0 us
  other arithmetic: 6.56 us -> 0 us
  local copies, waits for them, and re-layouts: 6.25 us -> 1.47 us
    pallas_call x0 -> x1, Pallas kernels: none -> 81.9 us  [on_device(): pl.pallas_call(functools.partial(kernel, n, unroll), out_shape=jax.ShapeD...]
    all_gather x3 -> x0, blocking collectives: 40.7 us -> none  [the longest x1 14 us: on_device(): lax.all_gather(queries, 'seq', axis=0, tiled=True)]
    dot_general x4 -> x0, matrix products: 13.6 us -> none  [the longest x1 6.94 us: on_device(): jnp.einsum('pkgd,pktd->pkgt', slot_queries, keys, preferred_element_type=...]
    all_to_all x3 -> x0, starting transfers between devices: 11.8 us -> none  [the longest x1 5.04 us: on_device(): lax.all_to_all(request_max, 'seq', split_axis=0, concat_axis=0, tiled=True)]
    all_to_all x3 -> x0, waiting for transfers between devices: 10.6 us -> none  [the longest x1 7.67 us: on_device(): lax.all_to_all(request_out, 'seq', split_axis=0, concat_axis=0, tiled=True)]
    unnamed x1 -> x0, blocking collectives: 9.92 us -> none
    reduce_sum x5 -> x0, other arithmetic: 2.83 us -> none  [the longest x1 1.24 us: on_device(): jnp.sum(jnp.where(matches, live_count[None, :, :], 0), axis=(1, 2))]
    unnamed x8 -> x1, local copies, waits for them, and re-layouts: 3.88 us -> 1.47 us
  transfers between devices with their start and end apart: 3 -> 0, of which waited for: 2 -> 0; matrix products, arithmetic and copies ran while one was open for 11% -> 0% of each run, Pallas kernels for 0% -> 0%
where the time goes in v1:
time: 83.5 us; the launch traced here: 83.3 us
  Pallas kernels  81.9 us (98%)
  local copies, waits for them, and re-layouts  1.47 us (2%)
    pallas_call x1, Pallas kernels, on_device(): pl.pallas_call(functools.partial(kernel, n, unroll), out_shape=jax.ShapeD...  81.9 us

profile of v1, /device:TPU:0, one launch (start us, length us, event | category | flops | bytes accessed | tf_op | source)
XLA Modules:
  0.0 83.3 jit_solution(15611361632928084449)
XLA Ops:
  0.0 81.9 %paged.1 = bf16[8,32,128]{2,1,0:T(8,128)(2,1)} custom-call(s32[8]{0:T(128)} %lens_ref.1, bf16[8,32,128]{2,1,0:T(8,128)(2,1)} %q_ref.1, s32[8,128]{1,0:T(8,128)} %owner_ref.1, s32[8,128]{1,0:T(8,128)} %slot_ref.1, bf16[64,4,128,128]{3,2,1,0:T(8,128)(2,1)} %k_hbm.1, bf16[64,4,128,128]{3,2,1,0:T(8,128)(2,1)} %v_hbm.1), custom_call_target="tpu_custom_call" | custom-call | tf_op jit(solution)/shard_map/paged/pallas_call | solution.py:267
  81.9 1.5 %copy.8 = bf16[8,32,128]{2,1,0:T(8,128)(2,1)} copy(bf16[8,32,128]{2,1,0:T(8,128)(2,1)} %paged.1) | data formatting | bytes 131072

commit v2 on v1

--- a/solution.py
+++ b/solution.py
@@ -20,7 +20,7 @@
 
 def kernel(
     n, unroll, lens_ref, q_ref, owner_ref, slot_ref, k_hbm, v_hbm, out_ref,
-    kbuf, vbuf, qall, tsend, trecv, liveb, reqb, mt, m, qslot, pmb, lb, oacc, ohi,
+    kbuf, vbuf, qall, tsend, trecv, liveb, reqb, mt, m, qslot, pmb, lb, wbuf, ohi,
     osend, orecv, ssend, srecv,
     ksem, vsem, tss, trs, qss, qrs, oss, ors, sss, srs,
 ):
@@ -152,7 +152,6 @@
             qcopies[h, off].wait_recv()
         qslot[...] = jnp.dot(mt[...], qall[h], preferred_element_type=F32)
         kcopies[h].wait()
-        vcopies[h].wait()
 
         def pages(i, top):
             for u in range(unroll):
@@ -165,22 +164,24 @@
                 pm = jnp.max(s, axis=1, keepdims=True)
                 w = jnp.exp(s - pm)
                 total = jnp.sum(w, axis=1, keepdims=True)
-                oacc[at, :] = jnp.dot(w.astype(BF16), vbuf[h, p], preferred_element_type=F32)
+                wbuf[at, :] = w
                 pmb[at, :] = jnp.broadcast_to(pm, (group, 128))
                 lb[at, :] = jnp.broadcast_to(total, (group, 128))
                 top = jnp.maximum(top, jnp.where(reqb[at, :] == lane_f + 1.0, pm, MASKED))
             return top
 
         top = lax.fori_loop(0, pool // unroll, pages, jnp.full((group, 128), MASKED, F32))
+        vcopies[h].wait()
 
         def merge(i, acc):
             for u in range(unroll):
                 p = i * unroll + u
                 at = pl.ds(pl.multiple_of(p * group, group), group)
+                out = jnp.dot(wbuf[at, :].astype(BF16), vbuf[h, p], preferred_element_type=F32)
                 mine = reqb[at, :] == lane_f + 1.0
                 rm = jnp.max(jnp.where(mine, top, MASKED), axis=1, keepdims=True)
                 sc = jnp.exp(jnp.minimum(pmb[at, :] - rm, 0.0))
-                ohi[at, :] = oacc[at, :] * sc
+                ohi[at, :] = out * sc
                 acc = acc + jnp.where(mine, sc * lb[at, :], 0.0)
             return acc
 

time: 83.5 us -> 33.3 us (0.40)
  Pallas kernels: 81.9 us -> 31.7 us
    pallas_call x1, Pallas kernels: 81.9 us -> 31.7 us  [on_device(): pl.pallas_call(functools.partial(kernel, n, unroll), out_shape=jax.ShapeD...]
where the time goes in v2:
time: 33.3 us; the launch traced here: 33.1 us
  Pallas kernels  31.7 us (95%)
  local copies, waits for them, and re-layouts  1.47 us (4%)
    pallas_call x1, Pallas kernels, on_device(): pl.pallas_call(functools.partial(kernel, n, unroll), out_shape=jax.ShapeD...  31.7 us
    unnamed x1, local copies, waits for them, and re-layouts  1.47 us

profile of v2, /device:TPU:0, one launch (start us, length us, event | category | flops | bytes accessed | tf_op | source)
XLA Modules:
  0.0 33.1 jit_solution(12891530724375483285)
XLA Ops:
  0.0 31.7 %paged.1 = bf16[8,32,128]{2,1,0:T(8,128)(2,1)} custom-call(s32[8]{0:T(128)} %lens_ref.1, bf16[8,32,128]{2,1,0:T(8,128)(2,1)} %q_ref.1, s32[8,128]{1,0:T(8,128)} %owner_ref.1, s32[8,128]{1,0:T(8,128)} %slot_ref.1, bf16[64,4,128,128]{3,2,1,0:T(8,128)(2,1)} %k_hbm.1, bf16[64,4,128,128]{3,2,1,0:T(8,128)(2,1)} %v_hbm.1), custom_call_target="tpu_custom_call" | custom-call | tf_op jit(solution)/shard_map/paged/pallas_call | solution.py:268
  31.7 1.5 %copy.8 = bf16[8,32,128]{2,1,0:T(8,128)(2,1)} copy(bf16[8,32,128]{2,1,0:T(8,128)(2,1)} %paged.1) | data formatting | bytes 131072
